TPU v7x, 32 devices: a whole 2x2x4 slice. The times are simulated.
32 devices in a mesh: dp: 4 (over z), expert: 4 (over y, x), tensor: 2 (over core).
Axes of the slice: x: 2, y: 2, z: 4, core: 2. Of those that a mesh axis runs over, the one named last changes fastest.
Arguments:
- tokens: bfloat16 [192, 7168], P(('dp', 'expert')), may hold values from -6 to 6
- expert_ids: int32 [192, 8], P(('dp', 'expert')), may hold values from 0 to 15, all different within a row; in each aligned block of 12 rows (0 to 11, 12 to 23, ...) at most 8 rows name the same one
- route_weights: float32 [192, 8], P(('dp', 'expert')), may hold values from 0.1 to 1
- gate_weights: bfloat16 [16, 7168, 2048], P('expert', 'dp', 'tensor'), may hold values from -0.0625 to 0.0625
- up_weights: bfloat16 [16, 7168, 2048], P('expert', 'dp', 'tensor'), may hold values from -0.0625 to 0.0625
- down_weights: bfloat16 [16, 2048, 7168], P('expert', 'tensor', 'dp'), may hold values from -0.125 to 0.125
- shared_gate: bfloat16 [7168, 2048], P('dp', 'tensor'), may hold values from -0.0625 to 0.0625
- shared_up: bfloat16 [7168, 2048], P('dp', 'tensor'), may hold values from -0.0625 to 0.0625
- shared_down: bfloat16 [2048, 7168], P('tensor', 'dp'), may hold values from -0.125 to 0.125
Outputs:
- mixed: bfloat16 [192, 7168], P(('dp', 'expert'))
Inputs may be any that keep to these rules, and one draw needn't show every extreme that they name: `expert_ids`: each token names 8 different experts. In the rows of one device no expert is named by more than 8 tokens, and in some device's rows some expert is named by exactly 8.
All inputs are finite; a program needn't handle non-finite values.
Results may differ from a plain program's by a relative error of at most 0.005.
Values may be sent and summed in bfloat16 or wider, within the bound.
A program may use at most 128 MiB of HBM per device.

v0:
```python
import jax
import jax.numpy as jnp
from jax import lax
from jax.sharding import PartitionSpec as P

EXPERTS = 16
CAP = 8


def build_slots(block_ids):
    expert_range = jnp.arange(EXPERTS, dtype=jnp.int32)
    marked = (block_ids[:, :, None] == expert_range[None, None, :]).astype(jnp.int32)
    per_token = jnp.sum(marked, axis=1)
    before = jnp.cumsum(per_token, axis=0) - per_token
    position = jnp.sum(marked * before[:, None, :], axis=2)
    return block_ids * CAP + position


def pack_rows(block_tokens, slot_block, slot_count):
    wanted = jnp.arange(slot_count, dtype=jnp.int32)
    picker = jnp.any(wanted[:, None, None] == slot_block[None, :, :], axis=2).astype(jnp.bfloat16)
    return jnp.dot(picker, block_tokens, preferred_element_type=jnp.float32).astype(jnp.bfloat16)


def gated(gate_full, up_full):
    return (jax.nn.silu(gate_full) * up_full).astype(jnp.bfloat16)


def combine_rows(returned, slot_ids, route_weights, shared_part):
    picked = jnp.take(returned, slot_ids, axis=0)
    extra = (1,) * (picked.ndim - 2)
    scaled = route_weights.reshape(route_weights.shape + extra) * picked
    return shared_part + jnp.sum(scaled, axis=1)


def per_device(
    tokens,
    expert_ids,
    route_weights,
    gate_weights,
    up_weights,
    down_weights,
    shared_gate,
    shared_up,
    shared_down,
):
    groups = lax.axis_size("expert")
    dp_count = lax.axis_size("dp")
    token_count = tokens.shape[0]
    model_width = tokens.shape[1]
    local_count = gate_weights.shape[0]
    block_width = gate_weights.shape[1]
    slot_ids = build_slots(expert_ids)
    outgoing = pack_rows(tokens, slot_ids, EXPERTS * CAP).reshape(
        groups, local_count * CAP, dp_count, block_width
    )
    arrived = lax.all_to_all(
        lax.all_to_all(outgoing, "dp", split_axis=2, concat_axis=2, tiled=True),
        "expert",
        split_axis=0,
        concat_axis=0,
        tiled=True,
    )
    own_columns = lax.all_to_all(
        tokens.reshape(token_count, dp_count, block_width),
        "dp",
        split_axis=1,
        concat_axis=1,
        tiled=True,
    )
    grouped = arrived.reshape(groups, local_count, CAP, dp_count, block_width)
    gate_part = jnp.einsum(
        "glcpd,ldf->glcpf", grouped, gate_weights, preferred_element_type=jnp.float32
    )
    up_part = jnp.einsum(
        "glcpd,ldf->glcpf", grouped, up_weights, preferred_element_type=jnp.float32
    )
    shared_gate_part = jnp.einsum(
        "tpd,df->tpf", own_columns, shared_gate, preferred_element_type=jnp.float32
    )
    shared_up_part = jnp.einsum(
        "tpd,df->tpf", own_columns, shared_up, preferred_element_type=jnp.float32
    )
    shared_gate_part = shared_gate_part.reshape(token_count, 1, 1, dp_count, -1)
    shared_up_part = shared_up_part.reshape(token_count, 1, 1, dp_count, -1)
    gate_full, up_full, shared_gate_full, shared_up_full = lax.psum(
        (gate_part, up_part, shared_gate_part, shared_up_part), "dp"
    )
    hidden = gated(gate_full, up_full)
    shared_hidden = gated(shared_gate_full, shared_up_full)
    routed_down = jnp.einsum(
        "glcpf,lfd->glcpd", hidden, down_weights, preferred_element_type=jnp.float32
    )
    shared_down_part = jnp.einsum(
        "tabpf,fd->tabpd", shared_hidden, shared_down, preferred_element_type=jnp.float32
    )
    routed_half, shared_half = (
        lax.psum_scatter(routed_down, "tensor", scatter_dimension=4, tiled=True),
        lax.psum_scatter(shared_down_part, "tensor", scatter_dimension=4, tiled=True),
    )
    half_width = routed_half.shape[4]
    results = routed_half.reshape(groups, local_count * CAP, dp_count, half_width)
    returned = lax.all_to_all(
        lax.all_to_all(results, "dp", split_axis=2, concat_axis=2, tiled=True),
        "expert",
        split_axis=0,
        concat_axis=0,
        tiled=True,
    ).reshape(EXPERTS * CAP, dp_count, half_width)
    shared_rows = shared_half.reshape(token_count, dp_count, half_width)
    shared_back = lax.all_to_all(shared_rows, "dp", split_axis=1, concat_axis=1, tiled=True)
    mixed_half = combine_rows(returned, slot_ids, route_weights, shared_back).astype(jnp.bfloat16)
    mixed_rows = lax.all_gather(mixed_half, "tensor", axis=2, tiled=True).reshape(
        token_count, model_width
    )
    return mixed_rows


def solution(mesh):
    placed = (
        P(("dp", "expert"), None),
        P(("dp", "expert"), None),
        P(("dp", "expert"), None),
        P("expert", "dp", "tensor"),
        P("expert", "dp", "tensor"),
        P("expert", "tensor", "dp"),
        P("dp", "tensor"),
        P("dp", "tensor"),
        P("tensor", "dp"),
    )
    return jax.shard_map(
        per_device, mesh=mesh, in_specs=placed, out_specs=P(("dp", "expert"), None), check_vma=False
    )
```

profile of v0, /device:TPU:0, one launch (start us, length us, event | category | flops | bytes accessed | tf_op | source)
XLA Modules:
  0.0 405.9 jit_solution(14784784320961439037)
XLA Ops:
  6.5 0.8 copy.84
  7.3 0.1 convert_reduce_fusion
  7.4 0.3 select_reduce_fusion
  7.8 0.1 fusion.35
  7.9 1.6 convolution_convert_fusion
  9.5 2.4 reshape.54
  11.9 3.0 copy.86
  14.9 6.5 %all-to-all-start.2 = ((bf16[4,32,4,1792]{3,1,0,2:T(8,128)(2,1)}), bf16[4,32,4,1792]{3,1,0,2:T(8,128)(2,1)S(1)}, u32[]{:S(2)}, u32[]{:S(2)}) async-start(bf16[4,32,4,1792]{3,1,0,2:T(8,128)(2,1)} %copy.86), calls=%async_computation.3 | async-start | bytes 3670016 | tf_op jit(solution)/shard_map/all_to_all | solution.py:58
  21.4 0.1 reshape.49
  21.5 0.7 copy.82
  22.2 41.8 %all-to-all-done.2 = bf16[4,32,4,1792]{3,1,0,2:T(8,128)(2,1)S(1)} async-done(((bf16[4,32,4,1792]{3,1,0,2:T(8,128)(2,1)}), bf16[4,32,4,1792]{3,1,0,2:T(8,128)(2,1)S(1)}, u32[]{:S(2)}, u32[]{:S(2)}) %all-to-all-start.2) | async-done | bytes 1835040 | tf_op jit(solution)/shard_map/all_to_all | solution.py:58
  63.9 3.4 all-to-all-start
  67.3 1.4 copy.87
  68.7 6.3 %all-to-all-done = bf16[12,4,1792]{2,0,1:T(8,128)(2,1)S(1)} async-done(((bf16[12,4,1792]{2,0,1:T(8,128)(2,1)}), bf16[12,4,1792]{2,0,1:T(8,128)(2,1)S(1)}, u32[]{:S(2)}, u32[]{:S(2)}) %all-to-all-start) | async-done | bytes 172064 | tf_op jit(solution)/shard_map/all_to_all | solution.py:64
  75.0 3.7 all-to-all-start.3
  78.8 3.7 fusion.26
  82.4 1.5 fusion.29
  83.9 14.1 %all-to-all-done.3 = bf16[4,32,4,1792]{3,1,2,0:T(8,128)(2,1)S(1)} async-done(((bf16[4,32,4,1792]{3,1,2,0:T(8,128)(2,1)}), bf16[4,32,4,1792]{3,1,2,0:T(8,128)(2,1)S(1)}, u32[]{:S(2)}, u32[]{:S(2)}) %all-to-all-start.3) | async-done | bytes 1835040 | tf_op jit(solution)/shard_map/all_to_all | solution.py:57
  97.9 8.6 %fusion.18 = f32[4,4,8,4,1024]{4,2,3,0,1:T(8,128)} fusion(bf16[4,1792,1024]{2,1,0:T(8,128)(2,1)} %param.12, bf16[4,32,4,1792]{3,1,2,0:T(8,128)(2,1)S(1)} %all-to-all-done.3), kind=kOutput, calls=%fused_computation.18 | convolution fusion | flops 1879048192 | bytes 18612224 | tf_op jit(solution)/shard_map/glcpd,ldf->glcpf/dot_general | solution.py:72
  106.6 8.6 %fusion.21 = f32[4,4,8,4,1024]{4,2,3,0,1:T(8,128)} fusion(bf16[4,1792,1024]{2,1,0:T(8,128)(2,1)} %param.13, bf16[4,32,4,1792]{3,1,2,0:T(8,128)(2,1)S(1)} %all-to-all-done.3), kind=kOutput, calls=%fused_computation.19 | convolution fusion | flops 1879048192 | bytes 18612224 | tf_op jit(solution)/shard_map/glcpd,ldf->glcpf/dot_general | solution.py:75
  115.2 0.0 all-reduce.3.cloned.1.call-update
  115.2 0.0 reduce-scatter.5.cloned.1.call-start
  115.2 172.6 %all-reduce.3.cloned.1.call-done = (f32[12,1,1,4,1024]{4,0,3,2,1:T(8,128)}, f32[12,1,1,4,1024]{4,0,3,2,1:T(8,128)}, f32[4,4,8,4,1024]{4,2,3,0,1:T(8,128)}, f32[4,4,8,4,1024]{4,2,3,0,1:T(8,128)}) async-done(((f32[12,1,1,4,1024]{4,0,3,2,1:T(8,128)}, f32[12,1,1,4,1024]{4,0,3,2,1:T(8,128)}, f32[4,4,8,4,1024]{4,2,3,0,1:T(8,128)}, f32[4,4,8,4,1024]{4,2,3,0,1:T(8,128)}), (f32[12,1,1,4,1024]{4,0,3,2,1:T(8,128)}, ...) | async-done | bytes 4587536 | tf_op jit(solution)/shard_map/psum | solution.py:86
  287.8 10.6 %fusion.12 = f32[4,4,8,4,1792]{4,2,3,0,1:T(8,128)} fusion(bf16[4,1024,1792]{2,1,0:T(8,128)(2,1)} %param.14, f32[4,4,8,4,1024]{4,2,3,0,1:T(8,128)} %get-tuple-element.7, f32[4,4,8,4,1024]{4,2,3,0,1:T(8,128)} %get-tuple-element.8), kind=kOutput, calls=%fused_computation.14 | convolution fusion | flops 1882193920 | bytes 22544384 | tf_op jit(solution)/shard_map/glcpf,lfd->glcpd/dot_general | solution.py:91
  298.4 0.0 reduce-scatter.5.cloned.1.call-update
  298.4 10.8 %reduce-scatter.5.cloned.1.call-done = f32[4,4,8,4,896]{4,2,3,0,1:T(8,128)} async-done(((f32[4,4,8,4,1792]{4,2,3,0,1:T(8,128)}), f32[4,4,8,4,896]{4,2,3,0,1:T(8,128)}) %reduce-scatter.5.cloned.1.call-update) | async-done | bytes 1835024 | tf_op jit(solution)/shard_map/reduce_scatter | solution.py:98
  309.2 1.7 copy.109
  310.9 0.1 copy.91
  311.0 47.7 %all_to_all.30 = f32[4,32,4,896]{3,1,0,2:T(8,128)S(1)} all-to-all(f32[4,32,4,896]{3,1,0,2:T(8,128)S(1)} %copy.91), channel_id=1, replica_groups=mesh['dp'=4,'expert'=4,'tensor'=2] {'dp'}, dimensions={2} | all-to-all | bytes 3670016 | tf_op jit(solution)/shard_map/all_to_all | solution.py:104
  358.7 1.4 copy.92
  360.0 3.8 all-to-all-start.5
  363.8 0.0 copy-start.4
  363.9 3.6 fusion.15
  367.4 0.0 reduce-scatter.3.cloned.1.call-update
  367.5 0.1 reshape.61
  367.5 7.5 %reduce-scatter.3.cloned.1.call-done = f32[12,1,1,4,896]{4,0,3,2,1:T(8,128)} async-done(((f32[12,1,1,4,1792]{4,0,3,2,1:T(8,128)}), f32[12,1,1,4,896]{4,0,3,2,1:T(8,128)}) %reduce-scatter.3.cloned.1.call-update) | async-done | bytes 172048 | tf_op jit(solution)/shard_map/reduce_scatter | solution.py:99
  375.0 10.3 %all-to-all-done.5 = f32[4,32,4,896]{3,1,2,0:T(8,128)S(1)} async-done(((f32[4,32,4,896]{3,1,2,0:T(8,128)}), f32[4,32,4,896]{3,1,2,0:T(8,128)S(1)}, u32[]{:S(2)}, u32[]{:S(2)}) %all-to-all-start.5) | async-done | bytes 1835040 | tf_op jit(solution)/shard_map/all_to_all | solution.py:103
  385.4 3.6 all-to-all-start.1
  388.9 0.1 copy.83
  389.0 0.1 copy.93
  389.2 1.2 copy.94
  390.4 1.4 gather_fusion
  391.8 0.5 multiply_reduce_fusion
  392.3 4.1 %all-to-all-done.1 = f32[12,4,896]{2,0,1:T(8,128)S(1)} async-done(((f32[12,4,896]{2,0,1:T(8,128)}), f32[12,4,896]{2,0,1:T(8,128)S(1)}, u32[]{:S(2)}, u32[]{:S(2)}) %all-to-all-start.1) | async-done | bytes 172064 | tf_op jit(solution)/shard_map/all_to_all | solution.py:111
  396.5 2.0 all_gather.3
  398.5 0.1 copy.96
  398.5 0.1 pad.1
  398.6 0.7 copy.100
  (17 shorter events, 0.1 us)
Async XLA Ops:
  14.9 6.5 %copy-start.1 = (bf16[12,7168]{1,0:T(8,128)(2,1)S(1)}, bf16[12,7168]{1,0:T(8,128)(2,1)}, u32[]{:S(2)}) copy-start(bf16[12,7168]{1,0:T(8,128)(2,1)} %param.9) | copy-start | bytes 516100
  14.9 49.1 %all-to-all-start.2 = ((bf16[4,32,4,1792]{3,1,0,2:T(8,128)(2,1)}), bf16[4,32,4,1792]{3,1,0,2:T(8,128)(2,1)S(1)}, u32[]{:S(2)}, u32[]{:S(2)}) async-start(bf16[4,32,4,1792]{3,1,0,2:T(8,128)(2,1)} %copy.86), calls=%async_computation.3 | async-start | bytes 3670016 | tf_op jit(solution)/shard_map/all_to_all | solution.py:58
  63.9 11.1 %all-to-all-start = ((bf16[12,4,1792]{2,0,1:T(8,128)(2,1)}), bf16[12,4,1792]{2,0,1:T(8,128)(2,1)S(1)}, u32[]{:S(2)}, u32[]{:S(2)}) async-start(bf16[12,4,1792]{2,0,1:T(8,128)(2,1)} %copy.82), calls=%async_computation | async-start | bytes 458752 | tf_op jit(solution)/shard_map/all_to_all | solution.py:64
  75.0 22.9 %all-to-all-start.3 = ((bf16[4,32,4,1792]{3,1,2,0:T(8,128)(2,1)}), bf16[4,32,4,1792]{3,1,2,0:T(8,128)(2,1)S(1)}, u32[]{:S(2)}, u32[]{:S(2)}) async-start(bf16[4,32,4,1792]{3,1,2,0:T(8,128)(2,1)} %copy.87), calls=%async_computation.4 | async-start | bytes 3670016 | tf_op jit(solution)/shard_map/all_to_all | solution.py:57
  78.8 209.0 %all-reduce.3.cloned.1.call-start = ((), (), s32[]{:S(2)}) async-start(), calls=%async_computation.10 | async-start | bytes 9437184 | tf_op jit(solution)/shard_map/psum | solution.py:86
  78.8 3.7 copy-start
  115.2 194.0 %reduce-scatter.5.cloned.1.call-start = ((), (), s32[]{:S(2)}) async-start(), calls=%async_computation.9 | async-start | bytes 5505024 | tf_op jit(solution)/shard_map/reduce_scatter | solution.py:98
  360.0 3.8 copy-start.2
  360.0 3.8 copy-start.3
  360.0 25.3 %all-to-all-start.5 = ((f32[4,32,4,896]{3,1,2,0:T(8,128)}), f32[4,32,4,896]{3,1,2,0:T(8,128)S(1)}, u32[]{:S(2)}, u32[]{:S(2)}) async-start(f32[4,32,4,896]{3,1,2,0:T(8,128)} %copy.92), calls=%async_computation.7 | async-start | bytes 3670016 | tf_op jit(solution)/shard_map/all_to_all | solution.py:103
  363.8 11.2 %reduce-scatter.3.cloned.1.call-start = ((), (), s32[]{:S(2)}) async-start(), calls=%async_computation.8 | async-start | bytes 688128 | tf_op jit(solution)/shard_map/reduce_scatter | solution.py:99
  363.8 25.1 %copy-start.4 = (f32[12,8]{0,1:T(8,128)S(1)}, f32[12,8]{0,1:T(8,128)}, u32[]{:S(2)}) copy-start(f32[12,8]{0,1:T(8,128)} %param.11) | copy-start | bytes 1156
  385.4 11.1 %all-to-all-start.1 = ((f32[12,4,896]{2,0,1:T(8,128)}), f32[12,4,896]{2,0,1:T(8,128)S(1)}, u32[]{:S(2)}, u32[]{:S(2)}) async-start(f32[12,4,896]{2,0,1:T(8,128)} %bitcast.75), calls=%async_computation.2 | async-start | bytes 458752 | tf_op jit(solution)/shard_map/all_to_all | solution.py:111
Sparse Core Ops, SparseCore 0:
  115.3 172.4 all-reduce.2
  298.5 10.6 reduce-scatter.4
  367.6 7.4 reduce-scatter.2
where the time goes:
time: 407 us; the launch traced here: 406 us
  waiting for transfers between devices  267 us (66%)
  blocking collectives  49.6 us (12%)
  matrix products  38.1 us (9%)
  starting transfers between devices  21 us (5%)
  local copies, waits for them, and re-layouts  15.3 us (4%)
  between operations  13.3 us (3%)
    psum x1, waiting for transfers between devices, per_device(): lax.psum((gate_part, up_part, shared_gate_part, shared_up_part), 'dp')  173 us
    all_to_all x1, blocking collectives, per_device(): lax.all_to_all(results, 'dp', split_axis=2, concat_axis=2, tiled=True)  47.7 us
    all_to_all x1, waiting for transfers between devices, per_device(): lax.all_to_all(outgoing, 'dp', split_axis=2, concat_axis=2, tiled=True)  41.8 us
    all_to_all x1, waiting for transfers between devices, per_device(): lax.all_to_all(lax.all_to_all(outgoing, 'dp', split_axis=2, concat_axis=2...  14.1 us
    reduce_scatter x1, waiting for transfers between devices, per_device(): lax.psum_scatter(routed_down, 'tensor', scatter_dimension=4, tiled=True)  10.8 us
    dot_general x1, matrix products, per_device(): jnp.einsum('glcpf,lfd->glcpd', hidden, down_weights, preferred_element_ty...  10.6 us
    all_to_all x1, waiting for transfers between devices, per_device(): lax.all_to_all(lax.all_to_all(results, 'dp', split_axis=2, concat_axis=2,...  10.3 us
    dot_general x1, matrix products, per_device(): jnp.einsum('glcpd,ldf->glcpf', grouped, gate_weights, preferred_element_t...  8.63 us
  transfers between devices with their start and end apart: 8, of which 8 were waited for; matrix products, arithmetic and copies ran while one was open for 4% of the time, Pallas kernels for 0%

commit v1 on v0

v1 whole, which is shorter than its diff:
```python
import functools

import jax
import jax.numpy as jnp
from jax import lax
from jax.experimental import pallas as pl
from jax.experimental.pallas import tpu as pltpu
from jax.sharding import PartitionSpec as P

CAP = 8
STEPS = 8
MESH = pl.DeviceIdType.MESH
VMEM = pl.BlockSpec(memory_space=pltpu.VMEM)
DMA = pltpu.SemaphoreType.DMA


def greet(peers):
    barrier = pltpu.get_barrier_semaphore()
    for peer in peers:
        pl.semaphore_signal(barrier, inc=1, device_id=peer, device_id_type=MESH)
    pl.semaphore_wait(barrier, len(peers))


def remote(src, dst, send, recv, peer):
    return pltpu.make_async_remote_copy(
        src_ref=src, dst_ref=dst, send_sem=send, recv_sem=recv, device_id=peer, device_id_type=MESH
    )


def params(number):
    return pltpu.CompilerParams(
        collective_id=number, has_side_effects=True, vmem_limit_bytes=60 * 1024 * 1024
    )


def squared(v):
    return v * jnp.abs(v)


def rooted(v):
    v = v.astype(jnp.float32)
    root = jnp.sqrt(jnp.abs(v))
    return jnp.where(v < 0.0, -root, root)


def dispatch_kernel(n, g, tok, coef, x, w, own, s1, r1, s2, r2):
    d, e = lax.axis_index("dp"), lax.axis_index("expert")
    greet(
        [{"dp": lax.rem(d + k, n)} for k in range(1, n)]
        + [{"expert": lax.rem(e + j, g)} for j in range(1, g)]
    )
    mine = [
        pltpu.make_async_copy(tok.at[d], x.at[d, e], own.at[0]),
        pltpu.make_async_copy(coef, w.at[d, e], own.at[1]),
    ]
    for copy in mine:
        copy.start()
    sends = []
    for k in range(1, n):
        to = lax.rem(d + k, n)
        for src, dst, a in ((tok.at[to], x.at[d, e], 0), (coef, w.at[d, e], 1)):
            copy = remote(src, dst, s1.at[a, k], r1.at[a, k], {"dp": to})
            copy.start()
            sends.append(copy)
    for k in range(n):
        block = lax.rem(d - k + n, n)
        for a, ref in ((0, x), (1, w)):
            if k == 0:
                mine[a].wait()
            else:
                remote(ref.at[block, e], ref.at[block, e], s1.at[a, k], r1.at[a, k], {"dp": d}).wait_recv()
            for j in range(1, g):
                copy = remote(
                    ref.at[block, e], ref.at[block, e], s2.at[a, k, j], r2.at[a, k, j],
                    {"expert": lax.rem(e + j, g)},
                )
                copy.start()
                sends.append(copy)
    for k in range(n):
        block = lax.rem(d - k + n, n)
        for a, ref in ((0, x), (1, w)):
            for j in range(1, g):
                at = ref.at[block, lax.rem(e - j + g, g)]
                remote(at, at, s2.at[a, k, j], r2.at[a, k, j], {"expert": e}).wait_recv()
    for copy in sends:
        copy.wait_send()


def dispatch(blocks, coef, n, g):
    return pl.pallas_call(
        functools.partial(dispatch_kernel, n, g),
        out_shape=(
            jax.ShapeDtypeStruct((n, g) + blocks.shape[1:], blocks.dtype),
            jax.ShapeDtypeStruct((n, g) + coef.shape, coef.dtype),
        ),
        in_specs=[VMEM] * 2,
        out_specs=(VMEM, VMEM),
        scratch_shapes=[
            DMA((2,)), DMA((2, n)), DMA((2, n)), DMA((2, n, g)), DMA((2, n, g)),
        ],
        compiler_params=params(0),
    )(blocks, coef)


def chain_kernel(
    n, steps, gate, up, scale, sgate, sup, hid, shid,
    got, out, sgot, sout, s1, r1, s2, r2, t1, q1, t2, q2,
):
    d = lax.axis_index("dp")
    prev, after = lax.rem(d - 1 + n, n), lax.rem(d + 1, n)
    greet([{"dp": prev}, {"dp": after}])
    place = (d, n - 1 - d)
    ahead = (jnp.minimum(d + 1, n - 1), jnp.maximum(d - 1, 0))
    behind = (jnp.maximum(d - 1, 0), jnp.minimum(d + 1, n - 1))

    routed = ((gate, up), got, out, hid, s1, r1, s2, r2)
    shared = ((sgate, sup), sgot, sout, shid, t1, q1, t2, q2)

    def partial_send(group, i, src, way):
        parts, got_, out_, hid_, sa, ra, sb, rb = group
        return [remote(src[h], got_.at[h, i], sa.at[h, i], ra.at[h, i], {"dp": ahead[way]}) for h in (0, 1)]

    def hidden_send(group, i, way):
        hid_, sb, rb = group[3], group[6], group[7]
        return remote(hid_.at[i], hid_.at[i], sb.at[i], rb.at[i], {"dp": behind[way]})

    def first(group, i, way):
        @pl.when(place[way] == 0)
        def _():
            for copy in partial_send(group, i, [part.at[i] for part in group[0]], way):
                copy.start()

    def forward(group, i, way, factor):
        parts, got_, out_, hid_ = group[:4]

        @pl.when(place[way] > 0)
        def _():
            for copy in partial_send(group, i, [got_.at[h, i] for h in (0, 1)], way):
                copy.wait_recv()
            sums = [rooted(parts[h][i]) + rooted(got_[h, i]) for h in (0, 1)]

            @pl.when(place[way] < n - 1)
            def _():
                for h in (0, 1):
                    out_[h, i] = squared(sums[h]).astype(out_.dtype)
                for copy in partial_send(group, i, [out_.at[h, i] for h in (0, 1)], way):
                    copy.start()

            @pl.when(place[way] == n - 1)
            def _():
                value = sums[0] / (1.0 + jnp.exp(-sums[0])) * sums[1]
                if factor is not None:
                    value = value * factor[i]
                hid_[i] = value.astype(hid_.dtype)
                hidden_send(group, i, way).start()

    def spread(group, i, way):
        hidden_send(group, i, way).wait_recv()

        @pl.when(place[way] > 0)
        def _():
            hidden_send(group, i, way).start()

    for s in range(steps):
        for way in (0, 1):
            first(routed, 2 * s + way, way)
    for way in (0, 1):
        first(shared, way, way)

    total = steps + 1
    for s in range(total + 2 * (n - 1)):
        for way in (0, 1):
            if s < steps:
                forward(routed, 2 * s + way, way, scale)
            elif s == steps:
                forward(shared, way, way, None)
            late = s - 2 * (n - 1 - place[way])

            @pl.when((place[way] < n - 1) & (late >= 0) & (late < steps))
            def _():
                spread(routed, 2 * late + way, way)

            @pl.when((place[way] < n - 1) & (late == steps))
            def _():
                spread(shared, way, way)

    def finish(group, i, way):
        parts, got_, out_ = group[:3]

        @pl.when(place[way] < n - 1)
        def _():
            for copy in partial_send(group, i, [out_.at[h, i] for h in (0, 1)], way):
                copy.wait_send()

        @pl.when(place[way] > 0)
        def _():
            hidden_send(group, i, way).wait_send()

    for s in range(steps):
        for way in (0, 1):
            finish(routed, 2 * s + way, way)
    for way in (0, 1):
        finish(shared, way, way)


def chain(gate, up, scale, sgate, sup, n):
    pieces, rows, width = gate.shape
    half, thin = sgate.shape[1:]
    wire = gate.dtype
    return pl.pallas_call(
        functools.partial(chain_kernel, n, pieces // 2),
        out_shape=(
            jax.ShapeDtypeStruct((pieces, rows, width), jnp.bfloat16),
            jax.ShapeDtypeStruct((2, half, thin), jnp.bfloat16),
        ),
        in_specs=[VMEM] * 5,
        out_specs=(VMEM, VMEM),
        scratch_shapes=[
            pltpu.VMEM((2, pieces, rows, width), wire),
            pltpu.VMEM((2, pieces, rows, width), wire),
            pltpu.VMEM((2, 2, half, thin), wire),
            pltpu.VMEM((2, 2, half, thin), wire),
            DMA((2, pieces)), DMA((2, pieces)), DMA((pieces,)), DMA((pieces,)),
            DMA((2, 2)), DMA((2, 2)), DMA((2,)), DMA((2,)),
        ],
        compiler_params=params(1),
    )(gate, up, scale, sgate, sup)


def collect_kernel(n, g, y, o, peer_in, z, plane, done, sa, ra, sb, rb, sc, rc, own):
    d, e, t = lax.axis_index("dp"), lax.axis_index("expert"), lax.axis_index("tensor")
    other = 1 - t
    half = n // 2
    greet(
        [{"tensor": other}]
        + [{"expert": lax.rem(e + j, g)} for j in range(1, g)]
        + [{"dp": lax.rem(d + k, n), "tensor": c} for k in range(1, n) for c in (0, 1)]
    )
    swap = []
    for j in range(g):
        to = lax.rem(e + j, g)
        copy = remote(
            y.at[pl.ds(other * half, half), to], peer_in.at[to], sa.at[j], ra.at[j], {"tensor": other}
        )
        copy.start()
        swap.append(copy)
    sends = []
    for j in list(range(1, g)) + [0]:
        to = lax.rem(e + j, g)
        swap[j].wait_recv()
        z[to] = y[pl.ds(t * half, half), to] + peer_in[to]
        if j:
            copy = remote(z.at[to], plane.at[j], sb.at[j], rb.at[j], {"expert": to})
            copy.start()
            sends.append(copy)
    total = z[e]
    for j in range(1, g):
        sends[j - 1].wait_recv()
        total = total + plane[j]
    done[...] = total.astype(done.dtype)
    last = []
    for i in range(half):
        home = t * half + i
        for c in (0, 1):
            here = (home == d) & (t == c)
            away = remote(
                done.at[i], o.at[d], sc.at[i, c], rc.at[d], {"dp": home, "tensor": c}
            )
            pl.when(jnp.logical_not(here))(away.start)
            local = pltpu.make_async_copy(done.at[i], o.at[d], own)
            pl.when(here)(local.start)
            last.append((here, away, local))
    for k in range(n):
        local_arrives = (d // half == t) & (d == k)

        @pl.when(jnp.logical_not(local_arrives))
        def _():
            remote(done.at[0], o.at[k], sc.at[0, 0], rc.at[k], {"dp": d}).wait_recv()

    for here, away, local in last:
        pl.when(jnp.logical_not(here))(away.wait_send)
        pl.when(here)(local.wait)
    for copy in swap + sends:
        copy.wait_send()


def collect(y, n, g):
    rows, width = y.shape[2:]
    half = n // 2
    return pl.pallas_call(
        functools.partial(collect_kernel, n, g),
        out_shape=jax.ShapeDtypeStruct((n, rows, width), jnp.bfloat16),
        in_specs=[VMEM],
        out_specs=VMEM,
        scratch_shapes=[
            pltpu.VMEM((g, half, rows, width), jnp.float32),
            pltpu.VMEM((g, half, rows, width), jnp.float32),
            pltpu.VMEM((g, half, rows, width), jnp.float32),
            pltpu.VMEM((half, rows, width), jnp.bfloat16),
            DMA((g,)), DMA((g,)), DMA((g,)), DMA((g,)), DMA((half, 2)), DMA((n,)), DMA,
        ],
        compiler_params=params(2),
    )(y)


def per_device(
    tokens, expert_ids, route_weights, gate_weights, up_weights, down_weights,
    shared_gate, shared_up, shared_down,
):
    g, n = lax.axis_size("expert"), lax.axis_size("dp")
    e = lax.axis_index("expert")
    rows, model = tokens.shape
    local, width, hidden = gate_weights.shape
    experts = local * g
    blocks = n * g
    count = blocks * rows
    wire = jnp.bfloat16 if n <= 4 else jnp.float32

    names = jnp.arange(experts, dtype=jnp.int32)
    coef = jnp.sum(
        jnp.where(expert_ids[:, :, None] == names, route_weights[:, :, None], 0.0), axis=1
    )
    x, w = dispatch(tokens.reshape(rows, n, width).transpose(1, 0, 2), coef, n, g)
    x = x.reshape(count, width)
    own = lax.dynamic_slice_in_dim(w.reshape(blocks, rows, experts), e * local, local, 2)
    chosen = own > 0.0
    order = jnp.tril(jnp.ones((rows, rows), jnp.float32), -1)
    place = jnp.einsum("ij,bjl->bil", order, chosen.astype(jnp.float32)).astype(jnp.int32)
    place = jnp.where(chosen, place, CAP).reshape(count, local)
    slot = jnp.arange(blocks * CAP, dtype=jnp.int32)
    block_of = jnp.arange(count, dtype=jnp.int32) // rows
    target = block_of[:, None] * CAP + place
    hit = (place < CAP).T[:, None, :] & (target.T[:, None, :] == slot[None, :, None])
    pick = hit.astype(jnp.bfloat16)
    scale = jnp.sum(jnp.where(hit, own.reshape(count, local).T[:, None, :], 0.0), axis=2)

    picked = jnp.einsum("lrt,td->lrd", pick, x, preferred_element_type=jnp.float32).astype(jnp.bfloat16)
    gate = squared(jnp.einsum("lrd,ldf->lrf", picked, gate_weights, preferred_element_type=jnp.float32)).astype(wire)
    up = squared(jnp.einsum("lrd,ldf->lrf", picked, up_weights, preferred_element_type=jnp.float32)).astype(wire)
    thin = hidden // g
    my_gate = lax.dynamic_slice_in_dim(shared_gate, e * thin, thin, 1)
    my_up = lax.dynamic_slice_in_dim(shared_up, e * thin, thin, 1)
    sgate = squared(jnp.dot(x, my_gate, preferred_element_type=jnp.float32)).astype(wire)
    sup = squared(jnp.dot(x, my_up, preferred_element_type=jnp.float32)).astype(wire)

    pieces = 2 * STEPS
    tall = local * blocks * CAP // pieces
    hid, shid = chain(
        gate.reshape(pieces, tall, hidden), up.reshape(pieces, tall, hidden),
        scale.reshape(pieces, tall, 1),
        sgate.reshape(2, count // 2, thin), sup.reshape(2, count // 2, thin), n,
    )
    hid = hid.reshape(local, blocks * CAP, hidden)
    shid = shid.reshape(count, thin)
    spread = jnp.einsum("lrt,lrf->tlf", pick, hid, preferred_element_type=jnp.float32).astype(jnp.bfloat16)
    my_down = lax.dynamic_slice_in_dim(shared_down, e * thin, thin, 0)
    y = jnp.dot(
        spread.reshape(count, local * hidden), down_weights.reshape(local * hidden, width),
        preferred_element_type=jnp.float32,
    ) + jnp.dot(shid, my_down, preferred_element_type=jnp.float32)
    o = collect(y.reshape(n, g, rows, width), n, g)
    return o.transpose(1, 0, 2).reshape(rows, model)


def solution(mesh):
    placed = (
        P(("dp", "expert"), None),
        P(("dp", "expert"), None),
        P(("dp", "expert"), None),
        P("expert", "dp", "tensor"),
        P("expert", "dp", "tensor"),
        P("expert", "tensor", "dp"),
        P("dp", "tensor"),
        P("dp", "tensor"),
        P("tensor", "dp"),
    )
    return jax.shard_map(
        per_device, mesh=mesh, in_specs=placed, out_specs=P(("dp", "expert"), None), check_vma=False
    )
```

time: 407 us -> 204 us (0.50)
  waiting for transfers between devices: 267 us -> 0 us
  Pallas kernels: 0 us -> 161 us
  blocking collectives: 49.6 us -> 0 us
  starting transfers between devices: 21 us -> 0 us
  between operations: 13.3 us -> 0.14 us
  matrix products: 38.1 us -> 27.8 us
    psum x1 -> x0, waiting for transfers between devices: 173 us -> none  [per_device(): lax.psum((gate_part, up_part, shared_gate_part, shared_up_part), 'dp')]
    pallas_call x0 -> x3, Pallas kernels: none -> 161 us  [the longest x1 115 us: chain(): pl.pallas_call(functools.partial(chain_kernel, n, pieces // 2), out_shape...]
    all_to_all x5 -> x0, waiting for transfers between devices: 76.6 us -> none  [the longest x1 41.8 us: per_device(): lax.all_to_all(outgoing, 'dp', split_axis=2, concat_axis=2, tiled=True)]
    all_to_all x1 -> x0, blocking collectives: 47.7 us -> none  [per_device(): lax.all_to_all(results, 'dp', split_axis=2, concat_axis=2, tiled=True)]
    all_to_all x5 -> x0, starting transfers between devices: 20.9 us -> none  [the longest x1 6.48 us: per_device(): lax.all_to_all(outgoing, 'dp', split_axis=2, concat_axis=2, tiled=True)]
    reduce_scatter x2 -> x0, waiting for transfers between devices: 18.3 us -> none  [the longest x1 10.8 us: per_device(): lax.psum_scatter(routed_down, 'tensor', scatter_dimension=4, tiled=True)]
    dot_general x7 -> x8, matrix products: 38.1 us -> 27.8 us  [the longest x1 9.08 us: per_device(): jnp.dot(spread.reshape(count, local * hidden), down_weights.reshape(local...]
  transfers between devices with their start and end apart: 8 -> 0, of which waited for: 8 -> 0; matrix products, arithmetic and copies ran while one was open for 4% -> 0% of each run, Pallas kernels for 0% -> 0%
where the time goes in v1:
time: 204 us; the launch traced here: 203 us
  Pallas kernels  161 us (79%)
  matrix products  27.8 us (14%)
  local copies, waits for them, and re-layouts  12.6 us (6%)
    pallas_call x1, Pallas kernels, chain(): pl.pallas_call(functools.partial(chain_kernel, n, pieces // 2), out_shape...  115 us
    pallas_call x1, Pallas kernels, collect(): pl.pallas_call(functools.partial(collect_kernel, n, g), out_shape=jax.Sha...  24.6 us
    pallas_call x1, Pallas kernels, dispatch(): pl.pallas_call(functools.partial(dispatch_kernel, n, g), out_shape=(jax.S...  21.9 us
    dot_general x1, matrix products, per_device(): jnp.dot(spread.reshape(count, local * hidden), down_weights.reshape(local...  9.08 us
    dot_general x1, matrix products, per_device(): jnp.einsum('lrd,ldf->lrf', picked, up_weights, preferred_element_type=jnp...  8.55 us

profile of v1, /device:TPU:0, one launch (start us, length us, event | category | flops | bytes accessed | tf_op | source)
XLA Modules:
  0.0 202.8 jit_solution(7880081497566514449)
XLA Ops:
  0.0 0.8 copy.20
  0.8 0.8 copy.21
  1.6 0.7 select_reduce_fusion.1.coef
  2.2 1.0 reshape.64
  3.3 0.7 copy.28
  4.0 21.9 %shard_map.91 = (bf16[4,4,12,1792]{3,2,1,0:T(8,128)(2,1)}, f32[4,4,12,16]{3,2,1,0:T(8,128)}) custom-call(bf16[4,12,1792]{2,1,0:T(8,128)(2,1)} %bitcast.48, f32[12,16]{1,0:T(8,128)} %select_reduce_fusion.1.coef), custom_call_target="tpu_custom_call" | custom-call | tf_op jit(solution)/shard_map/pallas_call | solution.py:90
  25.9 1.0 constant_dynamic-slice_fusion
  26.9 0.2 copy.25
  27.1 0.1 reshape.70
  27.2 0.2 fusion.4
  27.4 0.1 reshape.66
  27.5 0.4 select_reduce_fusion
  27.9 0.9 reshape.82.scale
  28.8 1.3 reshape.67
  30.1 1.3 reshape.79
  31.4 2.2 %fusion.21 = bf16[192,256]{1,0:T(8,128)(2,1)} fusion(bf16[192,1792]{1,0:T(8,128)(2,1)S(1)} %reshape.67, bf16[1792,1024]{1,0:T(8,128)(2,1)} %param.15, s32[]{:T(128)S(6)} %select_n.39), kind=kOutput, calls=%fused_computation.23 | convolution fusion | flops 176308224 | bytes 1703940 | tf_op jit(solution)/shard_map/dot_general | solution.py:343
  33.6 2.2 %fusion.16 = bf16[192,256]{1,0:T(8,128)(2,1)} fusion(bf16[192,1792]{1,0:T(8,128)(2,1)S(1)} %reshape.67, bf16[1792,1024]{1,0:T(8,128)(2,1)} %param.16, s32[]{:T(128)S(6)} %select_n.39), kind=kOutput, calls=%fused_computation.21 | convolution fusion | flops 176308224 | bytes 1703940 | tf_op jit(solution)/shard_map/dot_general | solution.py:344
  35.8 1.0 convolution_convert_fusion
  36.8 0.0 copy-start
  36.8 8.5 %fusion.1 = bf16[4,128,1024]{2,1,0:T(8,128)(2,1)} fusion(bf16[4,128,1792]{2,1,0:T(8,128)(2,1)S(1)} %convolution_convert_fusion, bf16[4,1792,1024]{2,1,0:T(8,128)(2,1)} %param.13), kind=kOutput, calls=%fused_computation.6 | convolution fusion | flops 1880621056 | bytes 17563648 | tf_op jit(solution)/shard_map/lrd,ldf->lrf/dot_general | solution.py:339
  45.3 1.2 copy-done
  46.5 3.1 %fusion = bf16[4,128,1024]{2,1,0:T(8,128)(2,1)} fusion(bf16[4,128,1792]{2,1,0:T(8,128)(2,1)S(1)} %convolution_convert_fusion, bf16[4,1792,1024]{2,1,0:T(8,128)(2,1)S(1)} %copy-done), kind=kOutput, calls=%fused_computation.5 | convolution fusion | flops 1880621056 | bytes 17563648 | tf_op jit(solution)/shard_map/lrd,ldf->lrf/dot_general | solution.py:338
  49.6 114.7 %shard_map.92 = (bf16[16,32,1024]{2,1,0:T(8,128)(2,1)}, bf16[2,96,256]{2,1,0:T(8,128)(2,1)}) custom-call(bf16[16,32,1024]{2,1,0:T(8,128)(2,1)} %bitcast.46, bf16[16,32,1024]{2,1,0:T(8,128)(2,1)} %bitcast.45, f32[16,32,1]{2,1,0:T(8,128)} %reshape.82.scale, bf16[2,96,256]{2,1,0:T(8,128)(2,1)} %bitcast.50, bf16[2,96,256]{2,1,0:T(8,128)(2,1)} %bitcast.51), custom_call_target="tpu_custom_call" | custom-call | tf_op jit(solution)/shard_map/pallas_call | solution.py:210
  164.3 0.0 copy-start.1
  164.3 9.1 %convolution_bitcast_fusion = f32[192,1792]{1,0:T(8,128)S(1)} fusion(bf16[4,1024,1792]{2,1,0:T(8,128)(2,1)} %param.14, bf16[4,128,1024]{2,1,0:T(8,128)(2,1)} %bitcast.55, s32[4,192]{1,0:T(4,128)S(1)} %add_bitcast_fusion, pred[4,192]{1,0:T(4,128)(4,1)S(1)} %compare_bitcast_fusion), kind=kOutput, calls=%fused_computation.4 | convolution fusion | flops 3020881920 | bytes 17108736 | tf_op jit(solution)/shard_map/dot_general | solution.py:357
  173.4 0.0 copy-done.1
  173.4 1.5 convolution_add_fusion
  175.0 1.4 reshape.76.y
  176.4 24.6 %shard_map.93 = bf16[4,12,1792]{2,1,0:T(8,128)(2,1)} custom-call(f32[4,4,12,1792]{3,2,1,0:T(8,128)} %reshape.76.y), custom_call_target="tpu_custom_call" | custom-call | tf_op jit(solution)/shard_map/pallas_call | solution.py:290
  201.0 1.0 copy.24
  202.0 0.1 pad
  202.1 0.7 copy.26
  (4 shorter events, 0.0 us)
Async XLA Ops:
  36.8 9.7 %copy-start = (bf16[4,1792,1024]{2,1,0:T(8,128)(2,1)S(1)}, bf16[4,1792,1024]{2,1,0:T(8,128)(2,1)}, u32[]{:S(2)}) copy-start(bf16[4,1792,1024]{2,1,0:T(8,128)(2,1)} %param.12) | copy-start | bytes 44040196
  164.3 9.1 %copy-start.1 = (bf16[2,96,256]{2,1,0:T(8,128)(2,1)S(1)}, bf16[2,96,256]{2,1,0:T(8,128)(2,1)}, u32[]{:S(2)}) copy-start(bf16[2,96,256]{2,1,0:T(8,128)(2,1)} %get-tuple-element.12) | copy-start | bytes 294916
